TPU v7x, 32 devices: a whole 2x2x4 slice. The times are simulated.
32 devices in a mesh: blk: 8 (over y, x, core), ulysses: 4 (over z).
Axes of the slice: x: 2, y: 2, z: 4, core: 2. Of those that a mesh axis runs over, the one named last changes fastest.
Arguments:
- tokens: bfloat16 [2048, 3072], P(('blk', 'ulysses')), may hold values from -6 to 6
- mod_shift: float32 [3072], replicated, may hold values from -3 to 3
- mod_scale: float32 [3072], replicated, may hold values from -3 to 3
- mod_gate: float32 [3072], replicated, may hold values from 0.5 to 1.5
- qkv_weight: bfloat16 [3, 3072, 3072], P(None, None, 'ulysses'), may hold values from -0.109375 to 0.109375
- query_gain: float32 [128], replicated, may hold values from 1 to 16
- key_gain: float32 [128], replicated, may hold values from 1 to 16
- out_weight: bfloat16 [3072, 3072], P(None, 'ulysses'), may hold values from -0.109375 to 0.109375
Outputs:
- mixed: bfloat16 [2048, 3072], P(('blk', 'ulysses'))
All inputs are finite; a program needn't handle non-finite values.
Results may differ from a plain program's by a relative error of at most 0.013.
The roundings to bfloat16 on the way count: a program that leaves them out, or rounds other values in their place, can miss the bound.
Values may be sent and summed in bfloat16 or wider, within the bound.
A program may use at most 128 MiB of HBM per device.

v0:
```python
import math

import jax
import jax.numpy as jnp
from jax import lax
from jax.sharding import PartitionSpec as P


def head_norm(projected, gain, factor):
    split = projected.reshape(projected.shape[0], -1, gain.shape[0])
    meansq = jnp.mean(split * split, axis=-1, keepdims=True)
    return (split * lax.rsqrt(meansq + 1e-06) * gain * factor).reshape(projected.shape)


def local(tokens, mod_shift, mod_scale, mod_gate, qkv_weight, query_gain, key_gain, out_weight):
    wide = tokens.astype(jnp.float32)
    center = jnp.mean(wide, axis=-1, keepdims=True)
    spread = jnp.mean((wide - center) ** 2, axis=-1, keepdims=True)
    normed = (wide - center) / jnp.sqrt(spread + 1e-06)
    modulated = (normed * (1.0 + mod_scale) + mod_shift).astype(jnp.bfloat16)
    head_size = query_gain.shape[0]
    local_width = qkv_weight.shape[2]
    heads_here = local_width // head_size
    factor = 1.0 / math.sqrt(head_size)
    sums = jnp.einsum(
        "rd,jde->jre",
        lax.all_gather(modulated, "ulysses", axis=0, tiled=True),
        qkv_weight,
        preferred_element_type=jnp.float32,
    )
    queries = head_norm(sums[0], query_gain, factor)
    keys = head_norm(sums[1], key_gain, 1.0)
    stacked = jnp.stack([queries, keys, sums[2]]).astype(jnp.bfloat16)
    queries, keys, values = (stacked[0], stacked[1], stacked[2])
    query_rows = queries.shape[0]
    query_heads = queries.reshape(query_rows, heads_here, head_size)
    start_state = (
        jnp.full((heads_here, query_rows), -1e30, jnp.float32),
        jnp.zeros((heads_here, query_rows), jnp.float32),
        jnp.zeros((heads_here, query_rows, head_size), jnp.float32),
    )
    key_part = lax.all_gather(keys, "blk", axis=0, tiled=True)
    value_part = lax.all_gather(values, "blk", axis=0, tiled=True)
    count = key_part.shape[0] // query_rows

    def step(position, state):
        highest, total, numerator = state
        key_block = lax.dynamic_slice_in_dim(key_part, position * query_rows, query_rows, 0)
        value_block = lax.dynamic_slice_in_dim(value_part, position * query_rows, query_rows, 0)
        key_block = key_block.reshape(query_rows, heads_here, head_size)
        value_block = value_block.reshape(query_rows, heads_here, head_size)
        scores = jnp.einsum(
            "qhd,khd->hqk", query_heads, key_block, preferred_element_type=jnp.float32
        )
        new_high = jnp.maximum(highest, jnp.max(scores, axis=-1))
        rescale = jnp.exp(highest - new_high)
        powers = jnp.exp(scores - new_high[..., None])
        total = total * rescale + jnp.sum(powers, axis=-1)
        numerator = numerator * rescale[..., None] + jnp.einsum(
            "hqk,khd->hqd",
            powers.astype(jnp.bfloat16),
            value_block,
            preferred_element_type=jnp.float32,
        )
        return (new_high, total, numerator)

    highest, total, numerator = lax.fori_loop(0, count, step, start_state)
    attended = (numerator / total[..., None]).transpose(1, 0, 2).reshape(query_rows, local_width)
    attended = attended.astype(jnp.bfloat16)
    columns = jnp.dot(
        lax.all_gather(attended, "ulysses", axis=1, tiled=True),
        out_weight,
        preferred_element_type=jnp.float32,
    )
    branch = lax.all_to_all(
        columns.astype(jnp.bfloat16), "ulysses", split_axis=0, concat_axis=1, tiled=True
    ).astype(columns.dtype)
    return (wide + mod_gate * branch).astype(jnp.bfloat16)


def solution(mesh):
    in_specs = (
        P(("blk", "ulysses"), None),
        P(),
        P(),
        P(),
        P(None, None, "ulysses"),
        P(),
        P(),
        P(None, "ulysses"),
    )
    out_specs = P(("blk", "ulysses"), None)
    return jax.shard_map(local, mesh=mesh, in_specs=in_specs, out_specs=out_specs, check_vma=False)
```

profile of v0, /device:TPU:0, one launch (start us, length us, event | category | flops | bytes accessed | tf_op | source)
XLA Modules:
  0.0 214.0 jit_solution(12685129563109106059)
XLA Ops:
  6.5 1.1 convert_reduce_fusion
  7.7 1.3 fusion.9
  9.0 0.7 broadcast_add_fusion
  9.7 2.0 fusion.12
  11.8 39.8 %all-gather.7.cloned.1.call-done = bf16[256,3072]{1,0:T(8,128)(2,1)} async-done(((bf16[64,3072]{1,0:T(8,128)(2,1)}), bf16[256,3072]{1,0:T(8,128)(2,1)}) %all-gather.7.cloned.1.call-update) | async-done | bytes 1572880 | tf_op jit(solution)/shard_map/all_gather | solution.py:27
  51.6 7.9 %convolution_bitcast_fusion = f32[3,256,768]{2,1,0:T(8,128)S(1)} fusion(bf16[3,3072,768]{2,1,0:T(8,128)(2,1)} %param.14, bf16[256,3072]{1,0:T(8,128)(2,1)} %all-gather.7.cloned.1.call-done), kind=kOutput, calls=%fused_computation.14 | convolution fusion | flops 3623878656 | bytes 18087936 | tf_op jit(solution)/shard_map/rd,jde->jre/dot_general | solution.py:25
  59.5 0.8 slice.32
  60.3 1.2 slice_multiply_fusion
  61.6 1.4 copy.30
  63.1 1.2 copy.31
  64.3 1.4 copy.28
  65.9 1.1 copy.29
  67.0 2.4 %multiply_convert_fusion = (bf16[1,256,768]{2,1,0:T(8,128)(2,1)S(1)}, bf16[1,256,768]{2,1,0:T(8,128)(2,1)}) fusion(f32[1,256,768]{2,1,0:T(8,128)} %copy.31, f32[3,256,768]{2,1,0:T(8,128)S(1)} %convolution_bitcast_fusion, f32[768]{0:T(1024)S(1)} %get-tuple-element.201, f32[768]{0:T(1024)S(1)} %get-tuple-element.202, f32[1,256,768]{2,1,0:T(8,128)} %copy.29), kind=kLoop, calls=%fused_computation.30 | loop fusion | flops 1376256 | bytes 3938304 | tf_op jit(solution)/shard_map/slice | solution.py:34
  69.9 21.6 %all-gather.13.cloned.1.call-done = bf16[1,2048,768]{2,1,0:T(8,128)(2,1)} async-done(((bf16[1,256,768]{2,1,0:T(8,128)(2,1)}), bf16[1,2048,768]{2,1,0:T(8,128)(2,1)}) %all-gather.13.cloned.1.call-update) | async-done | bytes 3145744 | tf_op jit(solution)/shard_map/all_gather | solution.py:43
  91.5 34.1 %all-gather.11.cloned.1.call-done = bf16[1,2048,768]{2,1,0:T(8,128)(2,1)} async-done(((bf16[1,256,768]{2,1,0:T(8,128)(2,1)}), bf16[1,2048,768]{2,1,0:T(8,128)(2,1)}) %all-gather.11.cloned.1.call-update) | async-done | bytes 3145744 | tf_op jit(solution)/shard_map/all_gather | solution.py:42
  125.6 23.6 %while.18 = (s32[]{:T(128)}, f32[6,256]{1,0:T(8,128)S(1)}, f32[6,256]{1,0:T(8,128)S(1)}, f32[6,256,128]{2,1,0:T(8,128)S(1)}, bf16[2048,768]{1,0:T(8,128)(2,1)}, ...) while((s32[]{:T(128)}, f32[6,256]{1,0:T(8,128)S(1)}, ...), condition=%wide.region_7.0_spmd.clone, body=%wide.region_4.0_spmd.clone.sunk | while | flops 203890176 | bytes 10715315 | solution.py:67
  125.6 1.2 constant_dynamic-slice_fusion.3
  127.8 0.7 convolution_add_fusion.2
  128.5 1.2 constant_dynamic-slice_fusion.3
  131.5 1.2 constant_dynamic-slice_fusion.3
  133.7 0.7 convolution_add_fusion.2
  134.4 1.2 constant_dynamic-slice_fusion.3
  137.4 1.2 constant_dynamic-slice_fusion.3
  140.3 1.2 constant_dynamic-slice_fusion.3
  143.3 1.2 constant_dynamic-slice_fusion.3
  146.2 1.2 constant_dynamic-slice_fusion.3
  149.4 0.8 divide_convert_fusion
  150.2 37.2 %all-gather.9.cloned.1.call-done = bf16[256,3072]{0,1:T(8,128)(2,1)} async-done(((bf16[256,768]{0,1:T(8,128)(2,1)}), bf16[256,3072]{0,1:T(8,128)(2,1)}) %all-gather.9.cloned.1.call-update) | async-done | bytes 1572880 | tf_op jit(solution)/shard_map/all_gather | solution.py:71
  187.4 4.2 %convolution_convert_fusion = bf16[256,768]{1,0:T(8,128)(2,1)S(1)} fusion(bf16[256,3072]{0,1:T(8,128)(2,1)} %all-gather.9.cloned.1.call-done, bf16[3072,768]{1,0:T(8,128)(2,1)} %param.17), kind=kOutput, calls=%fused_computation.16 | convolution fusion | flops 1208156160 | bytes 6684672 | tf_op jit(solution)/shard_map/dot_general | solution.py:70
  191.7 13.9 %all_to_all.13 = bf16[4,64,768]{2,1,0:T(8,128)(2,1)S(1)} all-to-all(bf16[4,64,768]{2,1,0:T(8,128)(2,1)S(1)} %bitcast.69), channel_id=1, replica_groups=mesh['blk'=8,'ulysses'=4] {'ulysses'}, dimensions={0} | all-to-all | bytes 786432 | tf_op jit(solution)/shard_map/all_to_all | solution.py:75
  205.7 0.9 copy-done
  206.6 0.8 fusion.13
  (94 shorter events, 13.5 us)
Async XLA Ops:
  6.5 45.1 %all-gather.7.cloned.1.call-start = ((), (), s32[]{:S(2)}) async-start(), calls=%async_computation.1 | async-start | bytes 1966080 | tf_op jit(solution)/shard_map/all_gather | solution.py:27
  11.7 48.6 %copy-start.2 = (f32[128]{0:T(128)S(1)}, f32[128]{0:T(128)}, u32[]{:S(2)}) copy-start(f32[128]{0:T(128)} %param.15) | copy-start | bytes 1540
  11.7 48.6 %copy-start.3 = (f32[128]{0:T(128)S(1)}, f32[128]{0:T(128)}, u32[]{:S(2)}) copy-start(f32[128]{0:T(128)} %param.16) | copy-start | bytes 1540
  11.7 79.8 %all-gather.13.cloned.1.call-start = ((), (), s32[]{:S(2)}) async-start(), calls=%async_computation.4 | async-start | bytes 3538944 | tf_op jit(solution)/shard_map/all_gather | solution.py:43
  60.3 65.3 %all-gather.11.cloned.1.call-start = ((), (), s32[]{:S(2)}) async-start(), calls=%async_computation.3 | async-start | bytes 3538944 | tf_op jit(solution)/shard_map/all_gather | solution.py:42
  69.4 118.0 %all-gather.9.cloned.1.call-start = ((), (), s32[]{:S(2)}) async-start(), calls=%async_computation.2 | async-start | bytes 1966080 | tf_op jit(solution)/shard_map/all_gather | solution.py:71
  205.6 1.0 copy-start
  205.6 1.0 copy-start.1
Sparse Core Ops, SparseCore 0:
  11.8 39.7 all-gather.6
  60.4 31.0 all-gather.12
  93.4 32.1 all-gather.10
  150.4 37.0 all-gather.8
where the time goes:
time: 215 us; the launch traced here: 214 us
  waiting for transfers between devices  133 us (62%)
  matrix products  21 us (10%)
  local copies, waits for them, and re-layouts  19.7 us (9%)
  blocking collectives  13.9 us (6%)
  between operations  13.3 us (6%)
  other arithmetic  12.5 us (6%)
    all_gather x1, waiting for transfers between devices, local(): lax.all_gather(modulated, 'ulysses', axis=0, tiled=True)  39.8 us
    all_gather x1, waiting for transfers between devices, local(): lax.all_gather(attended, 'ulysses', axis=1, tiled=True)  37.2 us
    all_gather x1, waiting for transfers between devices, local(): key_part = lax.all_gather(keys, 'blk', axis=0, tiled=True)  34.1 us
    all_gather x1, waiting for transfers between devices, local(): value_part = lax.all_gather(values, 'blk', axis=0, tiled=True)  21.6 us
    all_to_all x1, blocking collectives, local(): lax.all_to_all(columns.astype(jnp.bfloat16), 'ulysses', split_axis=0, con...  13.9 us
    dynamic_slice x16, local copies, waits for them, and re-layouts, step(): lax.dynamic_slice_in_dim(value_part, position * query_rows, query_rows, 0)  10.7 us
    dot_general x1, matrix products, local(): jnp.einsum('rd,jde->jre', lax.all_gather(modulated, 'ulysses', axis=0, ti...  7.86 us
    dot_general x8, matrix products, step(): jnp.einsum('hqk,khd->hqd', powers.astype(jnp.bfloat16), value_block, pref...  5.52 us
  transfers between devices with their start and end apart: 4, of which 4 were waited for; matrix products, arithmetic and copies ran while one was open for 4% of the time, Pallas kernels for 0%

commit v1 on v0

v1 whole, which is shorter than its diff:
```python
import functools
import math

import jax
import jax.numpy as jnp
from jax import lax
from jax.experimental import pallas as pl
from jax.experimental.pallas import tpu as pltpu
from jax.sharding import PartitionSpec as P

MESH = pl.DeviceIdType.MESH
BF = jnp.bfloat16
F32 = jnp.float32


def highest_bit(mask):
    return 1 << (mask.bit_length() - 1)


def lowest_bit(mask):
    return mask & -mask


def source_slot(mask, part):
    if mask & 1:
        return mask - 1, 1
    bit = highest_bit(mask) if part == 0 else lowest_bit(mask)
    return mask - bit, bit


def kernel(
    n_u, n_blk,
    tok_ref, shift_ref, scale_ref, gate_ref, w_hbm, qg_ref, kg_ref, wo_hbm, out_ref,
    w_ref, wo_ref, mod, q_ref, kv, att, stage, br,
    w_sem, sa_r, sa_l, ra, sb, rb, sc_r, sc_l, rc, sd, rd,
):
    z = lax.axis_index("ulysses")
    b = lax.axis_index("blk")
    rows, model = tok_ref.shape
    head = qg_ref.shape[1]
    width = w_ref.shape[2]
    heads = width // head
    factor = 1.0 / math.sqrt(head)
    last = n_u - 1
    bits = [1 << i for i in range(n_blk.bit_length() - 1)]
    pair = 2 if heads % 2 == 0 else heads
    tile = pair * head

    for j in (1, 2, 0):
        pltpu.make_async_copy(w_hbm.at[j], w_ref.at[j], w_sem.at[j]).start()
    pltpu.make_async_copy(wo_hbm, wo_ref, w_sem.at[3]).start()

    def flip(bit):
        return b + (1 - 2 * ((b // bit) % 2)) * bit

    barrier = pltpu.get_barrier_semaphore()
    for d in range(1, n_u):
        pl.semaphore_signal(
            barrier, inc=1, device_id={"ulysses": (z + d) % n_u}, device_id_type=MESH
        )
    for bit in bits:
        pl.semaphore_signal(barrier, inc=1, device_id={"blk": flip(bit)}, device_id_type=MESH)

    wide = tok_ref[...].astype(F32)
    center = jnp.mean(wide, axis=-1, keepdims=True)
    spread = jnp.mean((wide - center) ** 2, axis=-1, keepdims=True)
    normed = (wide - center) * lax.rsqrt(spread + 1e-06)
    mod[z] = (normed * (1.0 + scale_ref[...]) + shift_ref[...]).astype(BF)

    pl.semaphore_wait(barrier, n_u - 1 + len(bits))

    def line_copy(buf, index, send, recv, step):
        return pltpu.make_async_remote_copy(
            src_ref=buf.at[index], dst_ref=buf.at[index],
            send_sem=send.at[index], recv_sem=recv.at[index],
            device_id={"ulysses": z + step}, device_id_type=MESH,
        )

    def a_right(o):
        return line_copy(mod, o, sa_r, ra, 1)

    def a_left(o):
        return line_copy(mod, o, sa_l, ra, -1)

    def b_copy(mask, part, s):
        slot, bit = source_slot(mask, part)
        return pltpu.make_async_remote_copy(
            src_ref=kv.at[part, :, slot, s], dst_ref=kv.at[part, :, mask, s],
            send_sem=sb.at[mask, part, s], recv_sem=rb.at[mask, part, s],
            device_id={"blk": flip(bit)}, device_id_type=MESH,
        )

    masks = range(1, n_blk)

    def b_send(slot, part, s):
        for mask in sorted(masks, key=lambda m: m & 1):
            if source_slot(mask, part)[0] == slot:
                b_copy(mask, part, s).start()

    def b_level(level, s):
        for part in (0, 1):
            for mask in masks:
                if mask % 2 == 0 and bin(mask).count("1") == level:
                    b_copy(mask, part, s).wait_recv()
                    b_send(mask, part, s)

    levels = range(1, len(bits))

    def owner(s):
        near = jnp.minimum(z, last - z)
        k = (s + 1) // 2
        inner = jnp.where(s % 2 == 1, z - k, z + k)
        outer = jnp.where(z < last - z, z + s - near, z - s + near)
        return jnp.where(s <= 2 * near, inner, outer)

    def head_norm(sums, gain, scale):
        meansq = jnp.mean(sums * sums, axis=-1, keepdims=True)
        return sums * lax.rsqrt(meansq + 1e-06) * gain * scale

    def project(j, o, put):
        def body(i, _):
            start = pl.multiple_of(i * tile, tile)
            sums = jnp.dot(
                mod[o], w_ref[j, :, pl.ds(start, tile)], preferred_element_type=F32
            )
            for e in range(pair):
                put(i * pair + e, sums[:, e * head:(e + 1) * head])
            return 0

        lax.fori_loop(0, heads // pair, body, 0)

    def gather_step(s, _):
        o = owner(s)

        @pl.when(s > 0)
        def _():
            a_right(o).wait_recv()

        @pl.when((o <= z) & (z < last))
        def _():
            a_right(o).start()

        @pl.when((o >= z) & (z > 0))
        def _():
            a_left(o).start()

        def weights(j):
            @pl.when(s == 0)
            def _():
                pltpu.make_async_copy(w_hbm.at[j], w_ref.at[j], w_sem.at[j]).wait()

        def put_key(h, sums):
            kv[0, h, 0, s] = head_norm(sums, kg_ref[...], 1.0).astype(BF)

        def put_value(h, sums):
            kv[1, h, 0, s] = sums.astype(BF)

        def put_query(h, sums):
            q_ref[o, h] = head_norm(sums, qg_ref[...], factor).astype(BF)

        weights(1)
        project(1, o, put_key)
        b_send(0, 0, s)

        @pl.when(s > 0)
        def _():
            b_level(1, s - 1)

        weights(2)
        project(2, o, put_value)
        b_send(0, 1, s)

        @pl.when(s > 0)
        def _():
            for level in levels[1:]:
                b_level(level, s - 1)

        weights(0)
        project(0, o, put_query)
        return 0

    lax.fori_loop(0, n_u, gather_step, 0)
    for level in levels:
        b_level(level, last)

    def b_finish(s, _):
        for part in (0, 1):
            for mask in masks:
                if mask % 2 == 1:
                    b_copy(mask, part, s).wait_recv()
        return 0

    lax.fori_loop(0, n_u, b_finish, 0)
    pltpu.make_async_copy(wo_hbm, wo_ref, w_sem.at[3]).wait()

    keys_all = n_blk * n_u * rows

    def order(i):
        return jnp.where(i % 2 == 0, i // 2, last - i // 2)

    def c_right(o, src):
        return pltpu.make_async_remote_copy(
            src_ref=att.at[o, src], dst_ref=att.at[o, src],
            send_sem=sc_r.at[o, src], recv_sem=rc.at[o, src],
            device_id={"ulysses": z + 1}, device_id_type=MESH,
        )

    def c_left(o, src):
        return pltpu.make_async_remote_copy(
            src_ref=att.at[o, src], dst_ref=att.at[o, src],
            send_sem=sc_l.at[o, src], recv_sem=rc.at[o, src],
            device_id={"ulysses": z - 1}, device_id_type=MESH,
        )

    def d_copy(o, src):
        return pltpu.make_async_remote_copy(
            src_ref=stage.at[o], dst_ref=br.at[src],
            send_sem=sd.at[o], recv_sem=rd.at[src],
            device_id={"ulysses": o}, device_id_type=MESH,
        )

    def attend(o):
        for h in range(heads):
            keys = kv[0, h].reshape(keys_all, head)
            values = kv[1, h].reshape(keys_all, head)
            scores = lax.dot_general(
                q_ref[o, h], keys, (((1,), (1,)), ((), ())), preferred_element_type=F32
            )
            powers = jnp.exp(scores - jnp.max(scores, axis=-1, keepdims=True))
            total = jnp.sum(powers, axis=-1, keepdims=True)
            numerator = jnp.dot(powers.astype(BF), values, preferred_element_type=F32)
            att[o, z, :, h * head:(h + 1) * head] = (numerator / total).astype(BF)

    def mix_step(t, _):
        @pl.when(t < n_u)
        def _():
            o = order(t)
            attend(o)

            @pl.when(z < last)
            def _():
                c_right(o, z).start()

            @pl.when(z > 0)
            def _():
                c_left(o, z).start()

        for k in range(last, 0, -1):
            i = t - k

            @pl.when((i >= 0) & (i < n_u))
            def _():
                o = order(i)

                @pl.when(z - k >= 0)
                def _():
                    c_right(o, z - k).wait_recv()

                    @pl.when(z < last)
                    def _():
                        c_right(o, z - k).start()

                @pl.when(z + k <= last)
                def _():
                    c_left(o, z + k).wait_recv()

                    @pl.when(z > 0)
                    def _():
                        c_left(o, z + k).start()

        @pl.when(t >= last)
        def _():
            o = order(t - last)
            total = jnp.zeros((rows, width), F32)
            for src in range(n_u):
                total += jnp.dot(
                    att[o, src], wo_ref[src * width:(src + 1) * width, :],
                    preferred_element_type=F32,
                )

            @pl.when(o == z)
            def _():
                br[z] = total.astype(BF)

            @pl.when(o != z)
            def _():
                stage[o] = total.astype(BF)
                d_copy(o, z).start()

        return 0

    lax.fori_loop(0, n_u + last, mix_step, 0)

    for src in range(n_u):
        @pl.when(src != z)
        def _():
            d_copy(src, src).wait_recv()

        cols = slice(src * width, (src + 1) * width)
        out_ref[:, cols] = (
            tok_ref[:, cols].astype(F32) + gate_ref[:, cols] * br[src].astype(F32)
        ).astype(BF)

    def finish(s, _):
        @pl.when((s <= z) & (z < last))
        def _():
            a_right(s).wait_send()

        @pl.when((s >= z) & (z > 0))
        def _():
            a_left(s).wait_send()

        for src in range(n_u):
            @pl.when((src <= z) & (z < last))
            def _():
                c_right(s, src).wait_send()

            @pl.when((src >= z) & (z > 0))
            def _():
                c_left(s, src).wait_send()

        @pl.when(s != z)
        def _():
            d_copy(s, z).wait_send()

        for part in (0, 1):
            for mask in masks:
                b_copy(mask, part, s).wait_send()
        return 0

    lax.fori_loop(0, n_u, finish, 0)


def local(n_u, n_blk, tokens, mod_shift, mod_scale, mod_gate, qkv_weight, query_gain, key_gain, out_weight):
    rows, model = tokens.shape
    width = qkv_weight.shape[2]
    head = query_gain.shape[0]
    heads = width // head
    vmem = pl.BlockSpec(memory_space=pltpu.VMEM)
    hbm = pl.BlockSpec(memory_space=pl.ANY)
    dma = pltpu.SemaphoreType.DMA
    return pl.pallas_call(
        functools.partial(kernel, n_u, n_blk),
        out_shape=jax.ShapeDtypeStruct((rows, model), BF),
        in_specs=[vmem, vmem, vmem, vmem, hbm, vmem, vmem, hbm],
        out_specs=vmem,
        scratch_shapes=[
            pltpu.VMEM(qkv_weight.shape, BF),
            pltpu.VMEM(out_weight.shape, BF),
            pltpu.VMEM((n_u, rows, model), BF),
            pltpu.VMEM((n_u, heads, rows, head), BF),
            pltpu.VMEM((2, heads, n_blk, n_u, rows, head), BF),
            pltpu.VMEM((n_u, n_u, rows, width), BF),
            pltpu.VMEM((n_u, rows, width), BF),
            pltpu.VMEM((n_u, rows, width), BF),
            dma((4,)),
            dma((n_u,)), dma((n_u,)), dma((n_u,)),
            dma((n_blk, 2, n_u)), dma((n_blk, 2, n_u)),
            dma((n_u, n_u)), dma((n_u, n_u)), dma((n_u, n_u)),
            dma((n_u,)), dma((n_u,)),
        ],
        compiler_params=pltpu.CompilerParams(
            collective_id=0, has_side_effects=True, vmem_limit_bytes=66_000_000
        ),
    )(
        tokens, mod_shift[None], mod_scale[None], mod_gate[None],
        qkv_weight, query_gain[None], key_gain[None], out_weight,
    )


def solution(mesh):
    in_specs = (
        P(("blk", "ulysses"), None), P(), P(), P(),
        P(None, None, "ulysses"), P(), P(), P(None, "ulysses"),
    )
    out_specs = P(("blk", "ulysses"), None)
    body = functools.partial(local, mesh.shape["ulysses"], mesh.shape["blk"])
    return jax.shard_map(body, mesh=mesh, in_specs=in_specs, out_specs=out_specs, check_vma=False)
```

time: 215 us -> 101 us (0.47)
  waiting for transfers between devices: 133 us -> 0 us
  Pallas kernels: 0 us -> 98.9 us
  matrix products: 21 us -> 0 us
  local copies, waits for them, and re-layouts: 19.7 us -> 1.77 us
  blocking collectives: 13.9 us -> 0 us
  between operations: 13.3 us -> 0.01 us
  other arithmetic: 12.5 us -> 0 us
    all_gather x4 -> x0, waiting for transfers between devices: 133 us -> none  [the longest x1 39.8 us: local(): lax.all_gather(modulated, 'ulysses', axis=0, tiled=True)]
    pallas_call x0 -> x1, Pallas kernels: none -> 98.9 us  [local(): pl.pallas_call(functools.partial(kernel, n_u, n_blk), out_shape=jax.Shape...]
    dot_general x18 -> x0, matrix products: 21 us -> none  [the longest x1 7.86 us: local(): jnp.einsum('rd,jde->jre', lax.all_gather(modulated, 'ulysses', axis=0, ti...]
    all_to_all x1 -> x0, blocking collectives: 13.9 us -> none  [local(): lax.all_to_all(columns.astype(jnp.bfloat16), 'ulysses', split_axis=0, con...]
    dynamic_slice x24 -> x0, local copies, waits for them, and re-layouts: 12.1 us -> none  [the longest x16 10.7 us: step(): lax.dynamic_slice_in_dim(value_part, position * query_rows, query_rows, 0)]
    mul x7 -> x0, local copies, waits for them, and re-layouts: 5.22 us -> none  [the longest x2 2.79 us: head_norm(): meansq = jnp.mean(split * split, axis=-1, keepdims=True)]
    reduce_sum x12 -> x0, other arithmetic: 4.31 us -> none  [the longest x8 1.78 us: step(): total = total * rescale + jnp.sum(powers, axis=-1)]
    convert_element_type x3 -> x0, other arithmetic: 3.61 us -> none  [the longest x1 1.96 us: local(): modulated = (normed * (1.0 + mod_scale) + mod_shift).astype(jnp.bfloat16)]
  transfers between devices with their start and end apart: 4 -> 0, of which waited for: 4 -> 0; matrix products, arithmetic and copies ran while one was open for 4% -> 0% of each run, Pallas kernels for 0% -> 0%
where the time goes in v1:
time: 101 us
  Pallas kernels  98.9 us (98%)
  local copies, waits for them, and re-layouts  1.77 us (2%)
    pallas_call x1, Pallas kernels, local(): pl.pallas_call(functools.partial(kernel, n_u, n_blk), out_shape=jax.Shape...  98.9 us

profile of v1, /device:TPU:0, one launch (start us, length us, event | category | flops | bytes accessed | tf_op | source)
XLA Modules:
  0.0 100.7 jit_solution(10851283880356188279)
XLA Ops:
  0.0 98.9 %shard_map.82 = bf16[64,3072]{1,0:T(8,128)(2,1)} custom-call(bf16[64,3072]{1,0:T(8,128)(2,1)} %tok_ref.1, f32[1,3072]{1,0:T(1,128)} %bitcast.5, f32[1,3072]{1,0:T(1,128)} %bitcast.6, f32[1,3072]{1,0:T(1,128)} %bitcast.7, bf16[3,3072,768]{2,1,0:T(8,128)(2,1)} %w_hbm.1, f32[1,128]{1,0:T(1,128)} %bitcast.8, f32[1,128]{1,0:T(1,128)} %bitcast.9, ...), custom_call_target="tpu_custom_call" | custom-call | tf_op jit(solution)/shard_map/pallas_call | solution.py:342
  98.9 1.8 %copy.10 = bf16[64,3072]{1,0:T(8,128)(2,1)} copy(bf16[64,3072]{1,0:T(8,128)(2,1)} %shard_map.82) | data formatting | bytes 786432

commit v2 on v1

--- a/solution.py
+++ b/solution.py
@@ -42,6 +42,7 @@
     heads = width // head
     factor = 1.0 / math.sqrt(head)
     last = n_u - 1
+    half = rows // 2
     bits = [1 << i for i in range(n_blk.bit_length() - 1)]
     pair = 2 if heads % 2 == 0 else heads
     tile = pair * head
@@ -65,7 +66,8 @@
     center = jnp.mean(wide, axis=-1, keepdims=True)
     spread = jnp.mean((wide - center) ** 2, axis=-1, keepdims=True)
     normed = (wide - center) * lax.rsqrt(spread + 1e-06)
-    mod[z] = (normed * (1.0 + scale_ref[...]) + shift_ref[...]).astype(BF)
+    modulated = (normed * (1.0 + scale_ref[...]) + shift_ref[...]).astype(BF)
+    mod[pl.ds(2 * z, 2)] = modulated.reshape(2, half, model)
 
     pl.semaphore_wait(barrier, n_u - 1 + len(bits))
 
@@ -106,22 +108,17 @@
 
     levels = range(1, len(bits))
 
-    def owner(s):
-        near = jnp.minimum(z, last - z)
-        k = (s + 1) // 2
-        inner = jnp.where(s % 2 == 1, z - k, z + k)
-        outer = jnp.where(z < last - z, z + s - near, z - s + near)
-        return jnp.where(s <= 2 * near, inner, outer)
-
     def head_norm(sums, gain, scale):
         meansq = jnp.mean(sums * sums, axis=-1, keepdims=True)
         return sums * lax.rsqrt(meansq + 1e-06) * gain * scale
 
-    def project(j, o, put):
+    def project(j, first, count, put):
         def body(i, _):
             start = pl.multiple_of(i * tile, tile)
             sums = jnp.dot(
-                mod[o], w_ref[j, :, pl.ds(start, tile)], preferred_element_type=F32
+                mod[pl.ds(first, count)].reshape(count * half, model),
+                w_ref[j, :, pl.ds(start, tile)],
+                preferred_element_type=F32,
             )
             for e in range(pair):
                 put(i * pair + e, sums[:, e * head:(e + 1) * head])
@@ -129,59 +126,120 @@
 
         lax.fori_loop(0, heads // pair, body, 0)
 
-    def gather_step(s, _):
-        o = owner(s)
-
-        @pl.when(s > 0)
-        def _():
-            a_right(o).wait_recv()
-
-        @pl.when((o <= z) & (z < last))
-        def _():
-            a_right(o).start()
-
-        @pl.when((o >= z) & (z > 0))
-        def _():
-            a_left(o).start()
-
-        def weights(j):
-            @pl.when(s == 0)
-            def _():
+    def project_chunk(first, count, own=False):
+        units = pl.ds(first, count)
+
+        def ready(j):
+            if own:
                 pltpu.make_async_copy(w_hbm.at[j], w_ref.at[j], w_sem.at[j]).wait()
 
         def put_key(h, sums):
-            kv[0, h, 0, s] = head_norm(sums, kg_ref[...], 1.0).astype(BF)
+            keys = head_norm(sums, kg_ref[...], 1.0).astype(BF)
+            kv[0, h, 0, units] = keys.reshape(count, half, head)
 
         def put_value(h, sums):
-            kv[1, h, 0, s] = sums.astype(BF)
+            kv[1, h, 0, units] = sums.astype(BF).reshape(count, half, head)
 
         def put_query(h, sums):
-            q_ref[o, h] = head_norm(sums, qg_ref[...], factor).astype(BF)
-
-        weights(1)
-        project(1, o, put_key)
-        b_send(0, 0, s)
-
-        @pl.when(s > 0)
-        def _():
-            b_level(1, s - 1)
-
-        weights(2)
-        project(2, o, put_value)
-        b_send(0, 1, s)
-
-        @pl.when(s > 0)
-        def _():
-            for level in levels[1:]:
-                b_level(level, s - 1)
-
-        weights(0)
-        project(0, o, put_query)
-        return 0
-
-    lax.fori_loop(0, n_u, gather_step, 0)
-    for level in levels:
-        b_level(level, last)
+            queries = head_norm(sums, qg_ref[...], factor).astype(BF)
+            q_ref[h, units] = queries.reshape(count, half, head)
+
+        ready(1)
+        project(1, first, count, put_key)
+        for u in range(count):
+            b_send(0, 0, first + u)
+        ready(2)
+        project(2, first, count, put_value)
+        for u in range(count):
+            b_send(0, 1, first + u)
+        ready(0)
+        project(0, first, count, put_query)
+
+    for u in range(2):
+        @pl.when(z < last)
+        def _():
+            a_right(2 * z + u).start()
+
+        @pl.when(z > 0)
+        def _():
+            a_left(2 * z + u).start()
+
+    project_chunk(2 * z, 2, own=True)
+
+    def at_distance(k, act):
+        for side in (-1, 1):
+            o = z + side * k
+
+            @pl.when((o >= 0) & (o <= last))
+            def _():
+                act(o)
+
+    def pass_levels(which):
+        def act(o):
+            for level in which:
+                for u in range(2):
+                    b_level(level, 2 * o + u)
+        return act
+
+    def receive(k):
+        for u in range(2):
+            @pl.when(z - k >= 0)
+            def _():
+                a_right(2 * (z - k) + u).wait_recv()
+
+                @pl.when(z < last)
+                def _():
+                    a_right(2 * (z - k) + u).start()
+
+            @pl.when(z + k <= last)
+            def _():
+                a_left(2 * (z + k) + u).wait_recv()
+
+                @pl.when(z > 0)
+                def _():
+                    a_left(2 * (z + k) + u).start()
+
+    def previous(k, which):
+        if isinstance(k, int) and k == 1:
+            pass_levels(which)(z)
+        else:
+            at_distance(k - 1, pass_levels(which))
+
+    for k in range(1, last):
+        receive(k)
+        previous(k, levels[:1])
+        at_distance(k, lambda o: project_chunk(2 * o, 2))
+        previous(k, levels[1:])
+
+    ends = (z == 0) | (z == last)
+    far = last - z
+
+    def far_half(u):
+        @pl.when(ends)
+        def _():
+            @pl.when(z == 0)
+            def _():
+                a_left(2 * far + u).wait_recv()
+
+            @pl.when(z > 0)
+            def _():
+                a_right(2 * far + u).wait_recv()
+
+            project_chunk(2 * far + u, 1)
+
+    def far_levels(u, which):
+        @pl.when(ends)
+        def _():
+            for level in which:
+                b_level(level, 2 * far + u)
+
+    previous(last, levels[:1])
+    far_half(0)
+    previous(last, levels[1:])
+    far_levels(0, levels[:1])
+    far_half(1)
+    far_levels(0, levels[1:])
+    far_levels(1, levels)
 
     def b_finish(s, _):
         for part in (0, 1):
@@ -190,7 +248,7 @@
                     b_copy(mask, part, s).wait_recv()
         return 0
 
-    lax.fori_loop(0, n_u, b_finish, 0)
+    lax.fori_loop(0, 2 * n_u, b_finish, 0)
     pltpu.make_async_copy(wo_hbm, wo_ref, w_sem.at[3]).wait()
 
     keys_all = n_blk * n_u * rows
@@ -224,14 +282,30 @@
             keys = kv[0, h].reshape(keys_all, head)
             values = kv[1, h].reshape(keys_all, head)
             scores = lax.dot_general(
-                q_ref[o, h], keys, (((1,), (1,)), ((), ())), preferred_element_type=F32
+                q_ref[h, pl.ds(2 * o, 2)].reshape(rows, head), keys, (((1,), (1,)), ((), ())), preferred_element_type=F32
             )
             powers = jnp.exp(scores - jnp.max(scores, axis=-1, keepdims=True))
             total = jnp.sum(powers, axis=-1, keepdims=True)
             numerator = jnp.dot(powers.astype(BF), values, preferred_element_type=F32)
             att[o, z, :, h * head:(h + 1) * head] = (numerator / total).astype(BF)
 
-    def mix_step(t, _):
+    def pass_right(o, src):
+        c_right(o, src).wait_recv()
+
+        @pl.when(z < last)
+        def _():
+            c_right(o, src).start()
+
+    def pass_left(o, src):
+        c_left(o, src).wait_recv()
+
+        @pl.when(z > 0)
+        def _():
+            c_left(o, src).start()
+
+    low = z < n_u // 2
+
+    def attend_step(t, _):
         @pl.when(t < n_u)
         def _():
             o = order(t)
@@ -245,32 +319,39 @@
             def _():
                 c_left(o, z).start()
 
+        @pl.when((t > 0) & low & (z > 0))
+        def _():
+            pass_left(order(t - 1), z + 1)
+
+        @pl.when((t > 0) & jnp.logical_not(low) & (z < last))
+        def _():
+            pass_right(order(t - 1), z - 1)
+
+        return 0
+
+    lax.fori_loop(0, n_u + 1, attend_step, 0)
+
+    def mix_step(t, _):
         for k in range(last, 0, -1):
-            i = t - k
-
-            @pl.when((i >= 0) & (i < n_u))
-            def _():
-                o = order(i)
-
-                @pl.when(z - k >= 0)
-                def _():
-                    c_right(o, z - k).wait_recv()
-
-                    @pl.when(z < last)
-                    def _():
-                        c_right(o, z - k).start()
-
-                @pl.when(z + k <= last)
-                def _():
-                    c_left(o, z + k).wait_recv()
-
-                    @pl.when(z > 0)
-                    def _():
-                        c_left(o, z + k).start()
-
-        @pl.when(t >= last)
-        def _():
-            o = order(t - last)
+            i = t - k + 1
+            held = (i >= 0) & (i < n_u)
+            right_too = held & (z - k >= 0)
+            left_too = held & (z + k <= last)
+            if k == 1:
+                right_too = right_too & (low | (z == last))
+                left_too = left_too & (jnp.logical_not(low) | (z == 0))
+
+            @pl.when(right_too)
+            def _():
+                pass_right(order(i), z - k)
+
+            @pl.when(left_too)
+            def _():
+                pass_left(order(i), z + k)
+
+        @pl.when(t >= last - 1)
+        def _():
+            o = order(t - last + 1)
             total = jnp.zeros((rows, width), F32)
             for src in range(n_u):
                 total += jnp.dot(
@@ -289,7 +370,7 @@
 
         return 0
 
-    lax.fori_loop(0, n_u + last, mix_step, 0)
+    lax.fori_loop(0, n_u + last - 1, mix_step, 0)
 
     for src in range(n_u):
         @pl.when(src != z)
@@ -302,13 +383,14 @@
         ).astype(BF)
 
     def finish(s, _):
-        @pl.when((s <= z) & (z < last))
-        def _():
-            a_right(s).wait_send()
-
-        @pl.when((s >= z) & (z > 0))
-        def _():
-            a_left(s).wait_send()
+        for u in range(2):
+            @pl.when((s <= z) & (z < last))
+            def _():
+                a_right(2 * s + u).wait_send()
+
+            @pl.when((s >= z) & (z > 0))
+            def _():
+                a_left(2 * s + u).wait_send()
 
         for src in range(n_u):
             @pl.when((src <= z) & (z < last))
@@ -325,7 +407,8 @@
 
         for part in (0, 1):
             for mask in masks:
-                b_copy(mask, part, s).wait_send()
+                for u in range(2):
+                    b_copy(mask, part, 2 * s + u).wait_send()
         return 0
 
     lax.fori_loop(0, n_u, finish, 0)
@@ -347,15 +430,15 @@
         scratch_shapes=[
             pltpu.VMEM(qkv_weight.shape, BF),
             pltpu.VMEM(out_weight.shape, BF),
-            pltpu.VMEM((n_u, rows, model), BF),
-            pltpu.VMEM((n_u, heads, rows, head), BF),
-            pltpu.VMEM((2, heads, n_blk, n_u, rows, head), BF),
+            pltpu.VMEM((2 * n_u, rows // 2, model), BF),
+            pltpu.VMEM((heads, 2 * n_u, rows // 2, head), BF),
+            pltpu.VMEM((2, heads, n_blk, 2 * n_u, rows // 2, head), BF),
             pltpu.VMEM((n_u, n_u, rows, width), BF),
             pltpu.VMEM((n_u, rows, width), BF),
             pltpu.VMEM((n_u, rows, width), BF),
             dma((4,)),
-            dma((n_u,)), dma((n_u,)), dma((n_u,)),
-            dma((n_blk, 2, n_u)), dma((n_blk, 2, n_u)),
+            dma((2 * n_u,)), dma((2 * n_u,)), dma((2 * n_u,)),
+            dma((n_blk, 2, 2 * n_u)), dma((n_blk, 2, 2 * n_u)),
             dma((n_u, n_u)), dma((n_u, n_u)), dma((n_u, n_u)),
             dma((n_u,)), dma((n_u,)),
         ],

time: 101 us -> 89.4 us (0.89)
  Pallas kernels: 98.9 us -> 87.5 us
    pallas_call x1, Pallas kernels: 98.9 us -> 87.5 us  [local(): pl.pallas_call(functools.partial(kernel, n_u, n_blk), out_shape=jax.Shape...]
where the time goes in v2:
time: 89.4 us; the launch traced here: 89.2 us
  Pallas kernels  87.5 us (98%)
  local copies, waits for them, and re-layouts  1.77 us (2%)
    pallas_call x1, Pallas kernels, local(): pl.pallas_call(functools.partial(kernel, n_u, n_blk), out_shape=jax.Shape...  87.5 us

profile of v2, /device:TPU:0, one launch (start us, length us, event | category | flops | bytes accessed | tf_op | source)
XLA Modules:
  0.0 89.2 jit_solution(12512315886644614678)
XLA Ops:
  0.0 87.5 %shard_map.82 = bf16[64,3072]{1,0:T(8,128)(2,1)} custom-call(bf16[64,3072]{1,0:T(8,128)(2,1)} %tok_ref.1, f32[1,3072]{1,0:T(1,128)} %bitcast.5, f32[1,3072]{1,0:T(1,128)} %bitcast.6, f32[1,3072]{1,0:T(1,128)} %bitcast.7, bf16[3,3072,768]{2,1,0:T(8,128)(2,1)} %w_hbm.1, f32[1,128]{1,0:T(1,128)} %bitcast.8, f32[1,128]{1,0:T(1,128)} %bitcast.9, ...), custom_call_target="tpu_custom_call" | custom-call | tf_op jit(solution)/shard_map/pallas_call | solution.py:425
  87.5 1.8 %copy.10 = bf16[64,3072]{1,0:T(8,128)(2,1)} copy(bf16[64,3072]{1,0:T(8,128)(2,1)} %shard_map.82) | data formatting | bytes 786432

commit v3 on v2

--- a/solution.py
+++ b/solution.py
@@ -277,17 +277,24 @@
             device_id={"ulysses": o}, device_id_type=MESH,
         )
 
-    def attend(o):
+    group = 2 if n_u % 2 == 0 else 1
+
+    def attend(chunks):
         for h in range(heads):
             keys = kv[0, h].reshape(keys_all, head)
             values = kv[1, h].reshape(keys_all, head)
+            queries = jnp.concatenate(
+                [q_ref[h, pl.ds(2 * o, 2)].reshape(rows, head) for o in chunks], axis=0
+            )
             scores = lax.dot_general(
-                q_ref[h, pl.ds(2 * o, 2)].reshape(rows, head), keys, (((1,), (1,)), ((), ())), preferred_element_type=F32
+                queries, keys, (((1,), (1,)), ((), ())), preferred_element_type=F32
             )
             powers = jnp.exp(scores - jnp.max(scores, axis=-1, keepdims=True))
             total = jnp.sum(powers, axis=-1, keepdims=True)
             numerator = jnp.dot(powers.astype(BF), values, preferred_element_type=F32)
-            att[o, z, :, h * head:(h + 1) * head] = (numerator / total).astype(BF)
+            result = (numerator / total).astype(BF)
+            for g, o in enumerate(chunks):
+                att[o, z, :, h * head:(h + 1) * head] = result[g * rows:(g + 1) * rows]
 
     def pass_right(o, src):
         c_right(o, src).wait_recv()
@@ -306,30 +313,31 @@
     low = z < n_u // 2
 
     def attend_step(t, _):
-        @pl.when(t < n_u)
-        def _():
-            o = order(t)
-            attend(o)
-
-            @pl.when(z < last)
-            def _():
-                c_right(o, z).start()
-
-            @pl.when(z > 0)
-            def _():
-                c_left(o, z).start()
-
-        @pl.when((t > 0) & low & (z > 0))
-        def _():
-            pass_left(order(t - 1), z + 1)
-
-        @pl.when((t > 0) & jnp.logical_not(low) & (z < last))
-        def _():
-            pass_right(order(t - 1), z - 1)
+        @pl.when(t < n_u // group)
+        def _():
+            chunks = [order(group * t + g) for g in range(group)]
+            attend(chunks)
+            for o in chunks:
+                @pl.when(z < last)
+                def _():
+                    c_right(o, z).start()
+
+                @pl.when(z > 0)
+                def _():
+                    c_left(o, z).start()
+
+        for g in range(group):
+            @pl.when((t > 0) & low & (z > 0))
+            def _():
+                pass_left(order(group * (t - 1) + g), z + 1)
+
+            @pl.when((t > 0) & jnp.logical_not(low) & (z < last))
+            def _():
+                pass_right(order(group * (t - 1) + g), z - 1)
 
         return 0
 
-    lax.fori_loop(0, n_u + 1, attend_step, 0)
+    lax.fori_loop(0, n_u // group + 1, attend_step, 0)
 
     def mix_step(t, _):
         for k in range(last, 0, -1):

time: 89.4 us -> 88.4 us (0.989)
  Pallas kernels: 87.5 us -> 86.4 us
    pallas_call x1, Pallas kernels: 87.5 us -> 86.4 us  [local(): pl.pallas_call(functools.partial(kernel, n_u, n_blk), out_shape=jax.Shape...]
where the time goes in v3:
time: 88.4 us; the launch traced here: 88.2 us
  Pallas kernels  86.4 us (98%)
  local copies, waits for them, and re-layouts  1.77 us (2%)
    pallas_call x1, Pallas kernels, local(): pl.pallas_call(functools.partial(kernel, n_u, n_blk), out_shape=jax.Shape...  86.4 us

profile of v3, /device:TPU:0, one launch (start us, length us, event | category | flops | bytes accessed | tf_op | source)
XLA Modules:
  0.0 88.2 jit_solution(15057531912933960203)
XLA Ops:
  0.0 86.4 %shard_map.82 = bf16[64,3072]{1,0:T(8,128)(2,1)} custom-call(bf16[64,3072]{1,0:T(8,128)(2,1)} %tok_ref.1, f32[1,3072]{1,0:T(1,128)} %bitcast.5, f32[1,3072]{1,0:T(1,128)} %bitcast.6, f32[1,3072]{1,0:T(1,128)} %bitcast.7, bf16[3,3072,768]{2,1,0:T(8,128)(2,1)} %w_hbm.1, f32[1,128]{1,0:T(1,128)} %bitcast.8, f32[1,128]{1,0:T(1,128)} %bitcast.9, ...), custom_call_target="tpu_custom_call" | custom-call | tf_op jit(solution)/shard_map/pallas_call | solution.py:433
  86.4 1.8 %copy.10 = bf16[64,3072]{1,0:T(8,128)(2,1)} copy(bf16[64,3072]{1,0:T(8,128)(2,1)} %shard_map.82) | data formatting | bytes 786432
